TPU v7x, 128 devices: a whole 4x4x4 slice. The times are simulated.
128 devices in a mesh: lon: 32 (over z, y_lo, x), ch: 4 (over y_hi, core).
Axes of the slice: x: 4, y: 4 (y_hi: 2, y_lo: 2; y = y_hi * 2 + y_lo), z: 4, core: 2. Of those that a mesh axis runs over, the one named last changes fastest.
Arguments:
- grid_inputs: bfloat16 [921600, 474], P('lon'), may hold values from -6 to 6
- embed_weight: bfloat16 [474, 512], replicated, may hold values from -0.25 to 0.25
- embed_bias: float32 [512], replicated, may hold values from -3 to 3
- mesh_latent: bfloat16 [20480, 512], P('lon', 'ch'), may hold values from -6 to 6
- edge_features: bfloat16 [4, 720896], P(None, 'lon'), may hold values from -6 to 6
- senders: int32 [720896], P('lon'), may hold values from 0 to 921599, as said below
- receivers: int32 [720896], P('lon'), may hold values from 0 to 20479, as said below
- sender_weight: bfloat16 [512, 512], P(None, 'ch'), may hold values from -0.25 to 0.25
- receiver_weight: bfloat16 [512, 512], P(None, 'ch'), may hold values from -0.25 to 0.25
- feature_weight: bfloat16 [4, 512], P(None, 'ch'), may hold values from -3 to 3
- hidden_bias: float32 [512], P('ch'), may hold values from -3 to 3
- message_weight: bfloat16 [512, 512], P('ch'), may hold values from -0.25 to 0.25
- message_bias: float32 [512], replicated, may hold values from -1.2 to 1.2
- norm_gain: float32 [512], P('ch'), may hold values from 0.5 to 1.5
- norm_shift: float32 [512], P('ch'), may hold values from -3 to 3
Outputs:
- mesh_out: bfloat16 [20480, 512], P('lon', 'ch')
Inputs may be any that keep to these rules, and one draw needn't show every extreme that they name: Edge e belongs to block b = e // 22528. Its sender is c * 640 + t with latitude row t and a column c that lies, counted around the closed circle of 1440 columns, at most 4 columns before or after the block's own columns b * 45 to b * 45 + 44; some block reaches 4 columns on both sides. Within each aligned run of min(2048, 22528) edges of a block, the senders' columns, counted from the block's first widened column, lie within 7 consecutive columns. `receivers`: the receiver of edge e lies among the mesh nodes b * 640 to b * 640 + 639 of its block b = e // 22528; a mesh node may receive no edge.
All inputs are finite; a program needn't handle non-finite values.
Results may differ from a plain program's by a relative error of at most 0.0028.
Values may be sent and summed in bfloat16 or wider, within the bound.
No kernel may reach another device: no remote copies, remote signals or barrier semaphores. Data moves between devices by JAX's collectives and lax.ppermute only.
A program may use at most 128 MiB of HBM per device.

v0:
```python
import jax
import jax.numpy as jnp
from jax import lax
from jax.sharding import PartitionSpec as P

LAT = 640
HALO = 4


def with_halo(block, sides, width):
    for axis, dim in sides:
        count = lax.axis_size(axis)
        forward = [(i, i + 1) for i in range(count - 1)]
        forward.append((count - 1, 0))
        backward = [(target, source) for source, target in forward]
        low = lax.ppermute(
            lax.slice_in_dim(block, block.shape[dim] - width, None, axis=dim), axis, forward
        )
        high = lax.ppermute(lax.slice_in_dim(block, 0, width, axis=dim), axis, backward)
        block = jnp.concatenate([low, block, high], axis=dim)
    return block


def split_up(value, dim, devices):
    before, after = (value.shape[:dim], value.shape[dim + 1 :])
    return jnp.moveaxis(value.reshape(*before, devices, -1, *after), dim, 0)


def sent_and_summed(value, axis, dim):
    devices = lax.axis_size(axis)
    parts = lax.all_to_all(split_up(value, dim, devices), axis, 0, 0, tiled=True)
    return jnp.sum(parts, axis=0)


def embedded(grid_rows, embed_weight, embed_bias):
    return jax.nn.silu(
        jnp.dot(grid_rows, embed_weight, preferred_element_type=jnp.float32) + embed_bias
    ).astype(jnp.bfloat16)


def on_device(
    grid_inputs,
    embed_weight,
    embed_bias,
    mesh_latent,
    edge_features,
    senders,
    receivers,
    sender_weight,
    receiver_weight,
    feature_weight,
    hidden_bias,
    message_weight,
    message_bias,
    norm_gain,
    norm_shift,
):
    lon_count = lax.axis_size("lon")
    lon_place = lax.axis_index("lon")
    ch_place = lax.axis_index("ch")
    columns = grid_inputs.shape[0] // LAT
    mesh_nodes = mesh_latent.shape[0]
    share_width = mesh_latent.shape[1]
    full_width = message_weight.shape[1]
    latent = embedded(grid_inputs, embed_weight, embed_bias)
    own_terms = jnp.dot(latent, sender_weight, preferred_element_type=jnp.float32)
    widened = with_halo(
        own_terms.reshape(columns, LAT, share_width).astype(jnp.bfloat16), (("lon", 0),), HALO
    ).astype(jnp.float32)
    sent_terms = widened.reshape(-1, share_width)
    grid_column = senders // LAT
    shifted = jnp.mod(grid_column - lon_place * columns + HALO, columns * lon_count)
    local_send = shifted * LAT + senders % LAT
    local_recv = receivers - lon_place * mesh_nodes
    full_mesh = lax.all_gather(mesh_latent, "ch", axis=1, tiled=True)
    recv_terms = jnp.dot(full_mesh, receiver_weight, preferred_element_type=jnp.float32)
    edge_count = senders.shape[0]
    block_rows = min(2048, edge_count)
    steps_count = edge_count // block_rows
    feature_blocks = jnp.transpose(
        edge_features.reshape(edge_features.shape[0], steps_count, block_rows), (1, 0, 2)
    )
    node_ids = lax.broadcasted_iota(jnp.int32, (1, mesh_nodes), 1)

    def accumulate(carried, pieces):
        totals, tallies = carried
        send_ids, recv_ids, features = pieces
        before = jnp.take(sent_terms, send_ids, axis=0) + jnp.take(recv_terms, recv_ids, axis=0)
        before = (
            before
            + lax.dot_general(
                features,
                feature_weight,
                (((0,), (0,)), ((), ())),
                preferred_element_type=jnp.float32,
            )
            + hidden_bias
        )
        hidden = jax.nn.silu(before).astype(jnp.bfloat16)
        one_hot = (recv_ids[:, None] == node_ids).astype(jnp.bfloat16)
        totals = totals + lax.dot_general(
            one_hot, hidden, (((0,), (0,)), ((), ())), preferred_element_type=jnp.float32
        )
        tallies = tallies + jnp.sum(one_hot, axis=0, dtype=jnp.float32)
        return ((totals, tallies), None)

    start = (
        jnp.zeros((mesh_nodes, share_width), jnp.float32),
        jnp.zeros((mesh_nodes,), jnp.float32),
    )
    pieces_all = (
        local_send.reshape(steps_count, block_rows),
        local_recv.reshape(steps_count, block_rows),
        feature_blocks,
    )
    (totals, tallies), ignored = lax.scan(accumulate, start, pieces_all)
    partial_value = jnp.dot(
        totals, message_weight.astype(jnp.float32), precision=lax.Precision.HIGHEST
    )
    bias_share = lax.dynamic_slice_in_dim(message_bias, ch_place * share_width, share_width, 0)
    node_share = sent_and_summed(partial_value, "ch", 1) + tallies[:, None] * bias_share
    first_sum, second = lax.psum(
        (
            jnp.sum(node_share, axis=1, keepdims=True),
            jnp.sum(jnp.square(node_share), axis=1, keepdims=True),
        ),
        "ch",
    )
    centre = first_sum / full_width
    spread = second / full_width - jnp.square(centre)
    normed = (node_share - centre) * lax.rsqrt(spread + 1.0)
    return (mesh_latent.astype(jnp.float32) + normed * norm_gain + norm_shift).astype(jnp.bfloat16)


def solution(mesh):
    return jax.shard_map(
        on_device,
        mesh=mesh,
        in_specs=(
            P("lon", None),
            P(),
            P(),
            P("lon", "ch"),
            P(None, "lon"),
            P("lon"),
            P("lon"),
            P(None, "ch"),
            P(None, "ch"),
            P(None, "ch"),
            P("ch"),
            P("ch", None),
            P(),
            P("ch"),
            P("ch"),
        ),
        out_specs=P("lon", "ch"),
        check_vma=False,
    )
```

profile of v0, /device:TPU:1, one launch (start us, length us, event | category | flops | bytes accessed | tf_op | source)
XLA Modules:
  0.0 352.2 jit_solution(3035467392577934759)
XLA Ops:
  1.0 31.8 %multiply_convert_fusion.1 = bf16[28800,512]{1,0:T(8,128)(2,1)} fusion(bf16[28800,474]{0,1:T(8,128)(2,1)} %param.17, bf16[474,512]{1,0:T(8,128)(2,1)S(1)} %copy-done, f32[512]{0:T(512)} %param.19), kind=kOutput, calls=%fused_computation.33 | convolution fusion | flops 14067302400 | bytes 57281024 | tf_op jit(solution)/shard_map/dot_general | solution.py:37
  32.8 13.5 %convolution_convert_fusion = bf16[28800,128]{1,0:T(8,128)(2,1)S(1)} fusion(bf16[28800,512]{1,0:T(8,128)(2,1)} %multiply_convert_fusion.1, bf16[512,128]{1,0:T(8,128)(2,1)S(1)} %copy-done.4), kind=kOutput, calls=%fused_computation.34 | convolution fusion | flops 3778560000 | bytes 36995072 | tf_op jit(solution)/shard_map/dot_general | solution.py:66
  52.5 5.8 %collective-permute-start.1 = (bf16[4,640,128]{2,1,0:T(8,128)(2,1)}, bf16[4,640,128]{2,1,0:T(8,128)(2,1)S(1)}, u32[]{:S(2)}, u32[]{:S(2)}) collective-permute-start(bf16[4,640,128]{2,1,0:T(8,128)(2,1)} %bitcast.2), channel_id=1, source_target_pairs={{4,0},{8,4},{12,8},{16,12},{20,16},{24,20},{28,24},{32,28},{36,32}... | collective-permute-start | bytes 1966088 | tf_op jit(solution)/shard_map/ppermute | solution.py:19
  58.5 18.9 %all_gather.3 = bf16[640,512]{1,0:T(8,128)(2,1)S(1)} all-gather(bf16[640,128]{1,0:T(8,128)(2,1)S(1)} %copy-done.3), channel_id=1, replica_groups=mesh['lon'=32,'ch'=4] {'ch'}, dimensions={1}, use_global_device_ids=true | all-gather | bytes 819200 | tf_op jit(solution)/shard_map/all_gather | solution.py:75
  82.1 6.2 %bitcast_convert_fusion = f32[33920,128]{1,0:T(8,128)} fusion(bf16[53,640,128]{2,1,0:T(8,128)(2,1)S(1)} %pad_maximum_fusion), kind=kLoop, calls=%fused_computation.36 | loop fusion | flops 4341760 | bytes 26050560 | tf_op jit(solution)/shard_map/convert_element_type | solution.py:69
  88.3 231.8 %while.13 = (s32[]{:T(128)}, f32[640,128]{1,0:T(8,128)S(1)}, f32[640]{0:T(1024)S(1)}, s32[11,2048]{1,0:T(8,128)S(1)}, s32[11,2048]{1,0:T(8,128)S(1)}, /*index=5*...) while((s32[]{:T(128)}, f32[640,128]{1,0:T(8,128)S(1)}, ...), condition=%wide.region_2.3_spmd.clone, body=%wide.region_0.2_spmd.clone.sunk | while | flops 347021952 | bytes 7114884 | solution.py:116
  88.4 5.5 %gather_fusion = f32[2048,128]{1,0:T(8,128)S(1)} fusion(f32[640,128]{1,0:T(8,128)S(1)} %get-tuple-element.233, s32[2048]{0:T(1024)S(1)} %broadcast_clamp_fusion.4), kind=kCustom, calls=%fused_computation.1.clone.clone.1 | custom fusion | bytes 2105344 | tf_op jit(solution)/shard_map/while/body/eval_jaxpr/jit(_take)/gather | solution.py:88
  93.9 11.4 %gather_fusion.1 = f32[2048,128]{1,0:T(8,128)S(1)} fusion(f32[33920,128]{1,0:T(8,128)} %get-tuple-element.232, s32[2048]{0:T(1024)S(1)} %broadcast_clamp_fusion.5), kind=kCustom, calls=%fused_computation.clone.clone.1 | custom fusion | bytes 2105344 | tf_op jit(solution)/shard_map/while/body/eval_jaxpr/jit(_take)/gather | solution.py:88
  114.9 11.4 %gather_fusion.1 = f32[2048,128]{1,0:T(8,128)S(1)} fusion(f32[33920,128]{1,0:T(8,128)} %get-tuple-element.232, s32[2048]{0:T(1024)S(1)} %broadcast_clamp_fusion.5), kind=kCustom, calls=%fused_computation.clone.clone.1 | custom fusion | bytes 2105344 | tf_op jit(solution)/shard_map/while/body/eval_jaxpr/jit(_take)/gather | solution.py:88
  130.5 5.5 %gather_fusion = f32[2048,128]{1,0:T(8,128)S(1)} fusion(f32[640,128]{1,0:T(8,128)S(1)} %get-tuple-element.233, s32[2048]{0:T(1024)S(1)} %broadcast_clamp_fusion.4), kind=kCustom, calls=%fused_computation.1.clone.clone.1 | custom fusion | bytes 2105344 | tf_op jit(solution)/shard_map/while/body/eval_jaxpr/jit(_take)/gather | solution.py:88
  136.0 11.4 %gather_fusion.1 = f32[2048,128]{1,0:T(8,128)S(1)} fusion(f32[33920,128]{1,0:T(8,128)} %get-tuple-element.232, s32[2048]{0:T(1024)S(1)} %broadcast_clamp_fusion.5), kind=kCustom, calls=%fused_computation.clone.clone.1 | custom fusion | bytes 2105344 | tf_op jit(solution)/shard_map/while/body/eval_jaxpr/jit(_take)/gather | solution.py:88
  157.1 11.4 %gather_fusion.1 = f32[2048,128]{1,0:T(8,128)S(1)} fusion(f32[33920,128]{1,0:T(8,128)} %get-tuple-element.232, s32[2048]{0:T(1024)S(1)} %broadcast_clamp_fusion.5), kind=kCustom, calls=%fused_computation.clone.clone.1 | custom fusion | bytes 2105344 | tf_op jit(solution)/shard_map/while/body/eval_jaxpr/jit(_take)/gather | solution.py:88
  172.6 5.5 %gather_fusion = f32[2048,128]{1,0:T(8,128)S(1)} fusion(f32[640,128]{1,0:T(8,128)S(1)} %get-tuple-element.233, s32[2048]{0:T(1024)S(1)} %broadcast_clamp_fusion.4), kind=kCustom, calls=%fused_computation.1.clone.clone.1 | custom fusion | bytes 2105344 | tf_op jit(solution)/shard_map/while/body/eval_jaxpr/jit(_take)/gather | solution.py:88
  178.1 11.4 %gather_fusion.1 = f32[2048,128]{1,0:T(8,128)S(1)} fusion(f32[33920,128]{1,0:T(8,128)} %get-tuple-element.232, s32[2048]{0:T(1024)S(1)} %broadcast_clamp_fusion.5), kind=kCustom, calls=%fused_computation.clone.clone.1 | custom fusion | bytes 2105344 | tf_op jit(solution)/shard_map/while/body/eval_jaxpr/jit(_take)/gather | solution.py:88
  199.2 11.4 %gather_fusion.1 = f32[2048,128]{1,0:T(8,128)S(1)} fusion(f32[33920,128]{1,0:T(8,128)} %get-tuple-element.232, s32[2048]{0:T(1024)S(1)} %broadcast_clamp_fusion.5), kind=kCustom, calls=%fused_computation.clone.clone.1 | custom fusion | bytes 2105344 | tf_op jit(solution)/shard_map/while/body/eval_jaxpr/jit(_take)/gather | solution.py:88
  214.8 5.5 %gather_fusion = f32[2048,128]{1,0:T(8,128)S(1)} fusion(f32[640,128]{1,0:T(8,128)S(1)} %get-tuple-element.233, s32[2048]{0:T(1024)S(1)} %broadcast_clamp_fusion.4), kind=kCustom, calls=%fused_computation.1.clone.clone.1 | custom fusion | bytes 2105344 | tf_op jit(solution)/shard_map/while/body/eval_jaxpr/jit(_take)/gather | solution.py:88
  220.3 11.4 %gather_fusion.1 = f32[2048,128]{1,0:T(8,128)S(1)} fusion(f32[33920,128]{1,0:T(8,128)} %get-tuple-element.232, s32[2048]{0:T(1024)S(1)} %broadcast_clamp_fusion.5), kind=kCustom, calls=%fused_computation.clone.clone.1 | custom fusion | bytes 2105344 | tf_op jit(solution)/shard_map/while/body/eval_jaxpr/jit(_take)/gather | solution.py:88
  235.9 5.5 %gather_fusion = f32[2048,128]{1,0:T(8,128)S(1)} fusion(f32[640,128]{1,0:T(8,128)S(1)} %get-tuple-element.233, s32[2048]{0:T(1024)S(1)} %broadcast_clamp_fusion.4), kind=kCustom, calls=%fused_computation.1.clone.clone.1 | custom fusion | bytes 2105344 | tf_op jit(solution)/shard_map/while/body/eval_jaxpr/jit(_take)/gather | solution.py:88
  241.4 11.4 %gather_fusion.1 = f32[2048,128]{1,0:T(8,128)S(1)} fusion(f32[33920,128]{1,0:T(8,128)} %get-tuple-element.232, s32[2048]{0:T(1024)S(1)} %broadcast_clamp_fusion.5), kind=kCustom, calls=%fused_computation.clone.clone.1 | custom fusion | bytes 2105344 | tf_op jit(solution)/shard_map/while/body/eval_jaxpr/jit(_take)/gather | solution.py:88
  262.4 11.4 %gather_fusion.1 = f32[2048,128]{1,0:T(8,128)S(1)} fusion(f32[33920,128]{1,0:T(8,128)} %get-tuple-element.232, s32[2048]{0:T(1024)S(1)} %broadcast_clamp_fusion.5), kind=kCustom, calls=%fused_computation.clone.clone.1 | custom fusion | bytes 2105344 | tf_op jit(solution)/shard_map/while/body/eval_jaxpr/jit(_take)/gather | solution.py:88
  283.5 11.4 %gather_fusion.1 = f32[2048,128]{1,0:T(8,128)S(1)} fusion(f32[33920,128]{1,0:T(8,128)} %get-tuple-element.232, s32[2048]{0:T(1024)S(1)} %broadcast_clamp_fusion.5), kind=kCustom, calls=%fused_computation.clone.clone.1 | custom fusion | bytes 2105344 | tf_op jit(solution)/shard_map/while/body/eval_jaxpr/jit(_take)/gather | solution.py:88
  304.6 11.4 %gather_fusion.1 = f32[2048,128]{1,0:T(8,128)S(1)} fusion(f32[33920,128]{1,0:T(8,128)} %get-tuple-element.232, s32[2048]{0:T(1024)S(1)} %broadcast_clamp_fusion.5), kind=kCustom, calls=%fused_computation.clone.clone.1 | custom fusion | bytes 2105344 | tf_op jit(solution)/shard_map/while/body/eval_jaxpr/jit(_take)/gather | solution.py:88
  326.5 16.9 %all-to-all-done = f32[4,640,128]{1,2,0:T(8,128)S(1)} async-done(((f32[4,640,128]{1,2,0:T(8,128)}), f32[4,640,128]{1,2,0:T(8,128)S(1)}, u32[]{:S(2)}, u32[]{:S(2)}) %all-to-all-start) | async-done | bytes 1310752 | tf_op jit(solution)/shard_map/all_to_all | solution.py:31
  343.6 7.5 %all-reduce = (f32[640,1]{0,1:T(1,128)S(1)}, f32[640,1]{0,1:T(1,128)S(1)}) all-reduce(f32[640,1]{0,1:T(1,128)S(1)} %broadcast_in_dim.39, f32[640,1]{0,1:T(1,128)S(1)} %broadcast_in_dim.40), channel_id=1, replica_groups=mesh['lon'=32,'ch'=4] {'ch'}, use_global_device_ids=true, to_apply=%region_5.6 | all-reduce | flops 1280 | bytes 10240 | tf_op jit(solution)/shard_map/psum | solution.py:122
  (143 shorter events, 97.8 us)
Async XLA Ops:
  0.0 1.0 copy-start
  0.0 32.8 %copy-start.4 = (bf16[512,128]{1,0:T(8,128)(2,1)S(1)}, bf16[512,128]{1,0:T(8,128)(2,1)}, u32[]{:S(2)}) copy-start(bf16[512,128]{1,0:T(8,128)(2,1)} %param.24) | copy-start | bytes 393220
  32.8 25.4 %copy-start.7 = (s32[22528]{0:T(1024)S(1)}, s32[22528]{0:T(1024)}, u32[]{:S(2)}) copy-start(s32[22528]{0:T(1024)} %param.23) | copy-start | bytes 270340
  32.8 25.5 %copy-start.8 = (s32[22528]{0:T(1024)S(1)}, s32[22528]{0:T(1024)}, u32[]{:S(2)}) copy-start(s32[22528]{0:T(1024)} %param.22) | copy-start | bytes 270340
  32.8 25.7 %copy-start.3 = (bf16[640,128]{1,0:T(8,128)(2,1)S(1)}, bf16[640,128]{1,0:T(8,128)(2,1)}, u32[]{:S(2)}) copy-start(bf16[640,128]{1,0:T(8,128)(2,1)} %param.20) | copy-start | bytes 491524
  32.8 44.6 %copy-start.5 = (bf16[512,128]{1,0:T(8,128)(2,1)S(1)}, bf16[512,128]{1,0:T(8,128)(2,1)}, u32[]{:S(2)}) copy-start(bf16[512,128]{1,0:T(8,128)(2,1)} %param.25) | copy-start | bytes 393220
  46.3 3.0 copy-start.2
  50.4 27.3 %collective-permute-start = (bf16[4,640,128]{2,1,0:T(8,128)(2,1)}, bf16[4,640,128]{2,1,0:T(8,128)(2,1)S(1)}, u32[]{:S(2)}, u32[]{:S(2)}) collective-permute-start(bf16[4,640,128]{2,1,0:T(8,128)(2,1)} %bitcast), channel_id=1, source_target_pairs={{0,4},{4,8},{8,12},{12,16},{16,20},{20,24},{24,28},{28,32},{32,36}... | collective-permute-start | bytes 1966088 | tf_op jit(solution)/shard_map/ppermute | solution.py:16
  52.5 25.3 %collective-permute-start.1 = (bf16[4,640,128]{2,1,0:T(8,128)(2,1)}, bf16[4,640,128]{2,1,0:T(8,128)(2,1)S(1)}, u32[]{:S(2)}, u32[]{:S(2)}) collective-permute-start(bf16[4,640,128]{2,1,0:T(8,128)(2,1)} %bitcast.2), channel_id=1, source_target_pairs={{4,0},{8,4},{12,8},{16,12},{20,16},{24,20},{28,24},{32,28},{36,32}... | collective-permute-start | bytes 1966088 | tf_op jit(solution)/shard_map/ppermute | solution.py:19
  82.1 6.2 %copy-start.11 = (bf16[4,128]{1,0:T(4,128)(2,1)S(1)}, bf16[4,128]{1,0:T(4,128)(2,1)}, u32[]{:S(2)}) copy-start(bf16[4,128]{1,0:T(4,128)(2,1)} %param.26) | copy-start | bytes 3076
  82.1 6.2 %copy-start.12 = (f32[128]{0:T(128)S(1)}, f32[128]{0:T(128)}, u32[]{:S(2)}) copy-start(f32[128]{0:T(128)} %param.27) | copy-start | bytes 1540
  88.3 231.8 %copy-start.6 = (bf16[128,512]{1,0:T(8,128)(2,1)S(1)}, bf16[128,512]{1,0:T(8,128)(2,1)}, u32[]{:S(2)}) copy-start(bf16[128,512]{1,0:T(8,128)(2,1)} %param.28) | copy-start | bytes 393220
  88.3 262.9 %copy-start.9 = (f32[128]{0:T(128)S(1)}, f32[128]{0:T(128)}, u32[]{:S(2)}) copy-start(f32[128]{0:T(128)} %param.31) | copy-start | bytes 1540
  88.3 262.9 %copy-start.10 = (f32[128]{0:T(128)S(1)}, f32[128]{0:T(128)}, u32[]{:S(2)}) copy-start(f32[128]{0:T(128)} %param.30) | copy-start | bytes 1540
  320.1 32.1 %copy-start.1 = (bf16[474,512]{1,0:T(8,128)(2,1)S(1)}, bf16[474,512]{1,0:T(8,128)(2,1)}, u32[]{:S(2)}) copy-start(bf16[474,512]{1,0:T(8,128)(2,1)} %param.18) | copy-start | bytes 1456132
  321.9 21.4 %all-to-all-start = ((f32[4,640,128]{1,2,0:T(8,128)}), f32[4,640,128]{1,2,0:T(8,128)S(1)}, u32[]{:S(2)}, u32[]{:S(2)}) async-start(f32[4,640,128]{1,2,0:T(8,128)} %bitcast.7), calls=%async_computation | async-start | bytes 2621440 | tf_op jit(solution)/shard_map/all_to_all | solution.py:31
where the time goes:
time: 353 us; the launch traced here: 352 us
  local copies, waits for them, and re-layouts  193 us (55%)
  matrix products  84.4 us (24%)
  blocking collectives  26.4 us (7%)
  other arithmetic  19.2 us (5%)
  waiting for transfers between devices  16.9 us (5%)
  starting transfers between devices  11.4 us (3%)
    gather x11, local copies, waits for them, and re-layouts, accumulate(): jnp.take(sent_terms, send_ids, axis=0)  125 us
    gather x11, local copies, waits for them, and re-layouts, accumulate(): jnp.take(recv_terms, recv_ids, axis=0)  60.1 us
    dot_general x11, matrix products, accumulate(): lax.dot_general(one_hot, hidden, (((0,), (0,)), ((), ())), preferred_elem...  37.1 us
    dot_general x1, matrix products, embedded(): jnp.dot(grid_rows, embed_weight, preferred_element_type=jnp.float32)  31.8 us
    all_gather x1, blocking collectives, on_device(): full_mesh = lax.all_gather(mesh_latent, 'ch', axis=1, tiled=True)  18.9 us
    all_to_all x1, waiting for transfers between devices, sent_and_summed(): lax.all_to_all(split_up(value, dim, devices), axis, 0, 0, tiled=True)  16.9 us
    dot_general x1, matrix products, on_device(): jnp.dot(latent, sender_weight, preferred_element_type=jnp.float32)  13.5 us
    psum x1, blocking collectives, on_device(): lax.psum((jnp.sum(node_share, axis=1, keepdims=True), jnp.sum(jnp.square(...  7.53 us
  transfers between devices with their start and end apart: 3, of which 1 were waited for; matrix products, arithmetic and copies ran while one was open for 0% of the time, Pallas kernels for 0%

commit v1 on v0

--- a/solution.py
+++ b/solution.py
@@ -72,7 +72,8 @@
     shifted = jnp.mod(grid_column - lon_place * columns + HALO, columns * lon_count)
     local_send = shifted * LAT + senders % LAT
     local_recv = receivers - lon_place * mesh_nodes
-    full_mesh = lax.all_gather(mesh_latent, "ch", axis=1, tiled=True)
+    sent = jnp.stack([mesh_latent] * lax.axis_size("ch"))
+    full_mesh = jnp.concatenate(lax.all_to_all(sent, "ch", 0, 0), axis=1)
     recv_terms = jnp.dot(full_mesh, receiver_weight, preferred_element_type=jnp.float32)
     edge_count = senders.shape[0]
     block_rows = min(2048, edge_count)

time: 353 us -> 359 us (1.017)
  blocking collectives: 26.4 us -> 7.53 us
  waiting for transfers between devices: 16.9 us -> 32 us
  starting transfers between devices: 11.4 us -> 16.9 us
    all_gather x1 -> x0, blocking collectives: 18.9 us -> none  [on_device(): full_mesh = lax.all_gather(mesh_latent, 'ch', axis=1, tiled=True)]
    all_to_all x0 -> x1, waiting for transfers between devices: none -> 15 us  [on_device(): full_mesh = jnp.concatenate(lax.all_to_all(sent, 'ch', 0, 0), axis=1)]
    all_to_all x0 -> x1, starting transfers between devices: none -> 5.13 us  [on_device(): full_mesh = jnp.concatenate(lax.all_to_all(sent, 'ch', 0, 0), axis=1)]
  transfers between devices with their start and end apart: 3 -> 4, of which waited for: 1 -> 2; matrix products, arithmetic and copies ran while one was open for 0% -> 1% of each run, Pallas kernels for 0% -> 0%
where the time goes in v1:
time: 359 us; the launch traced here: 355 us
  local copies, waits for them, and re-layouts  194 us (54%)
  matrix products  84.5 us (24%)
  waiting for transfers between devices  32 us (9%)
  other arithmetic  19.2 us (5%)
  starting transfers between devices  16.9 us (5%)
  blocking collectives  7.53 us (2%)
    gather x11, local copies, waits for them, and re-layouts, accumulate(): jnp.take(sent_terms, send_ids, axis=0)  125 us
    gather x11, local copies, waits for them, and re-layouts, accumulate(): jnp.take(recv_terms, recv_ids, axis=0)  60.1 us
    dot_general x11, matrix products, accumulate(): lax.dot_general(one_hot, hidden, (((0,), (0,)), ((), ())), preferred_elem...  37.1 us
    dot_general x1, matrix products, embedded(): jnp.dot(grid_rows, embed_weight, preferred_element_type=jnp.float32)  31.7 us
    all_to_all x1, waiting for transfers between devices, sent_and_summed(): lax.all_to_all(split_up(value, dim, devices), axis, 0, 0, tiled=True)  17 us
    all_to_all x1, waiting for transfers between devices, on_device(): full_mesh = jnp.concatenate(lax.all_to_all(sent, 'ch', 0, 0), axis=1)  15 us
    dot_general x1, matrix products, on_device(): jnp.dot(latent, sender_weight, preferred_element_type=jnp.float32)  13.5 us
    psum x1, blocking collectives, on_device(): lax.psum((jnp.sum(node_share, axis=1, keepdims=True), jnp.sum(jnp.square(...  7.53 us
  transfers between devices with their start and end apart: 4, of which 2 were waited for; matrix products, arithmetic and copies ran while one was open for 1% of the time, Pallas kernels for 0%

profile of v1, /device:TPU:1, one launch (start us, length us, event | category | flops | bytes accessed | tf_op | source)
XLA Modules:
  0.0 354.9 jit_solution(12217390365969735245)
XLA Ops:
  1.0 31.7 %multiply_convert_fusion.1 = bf16[28800,512]{1,0:T(8,128)(2,1)} fusion(bf16[28800,474]{0,1:T(8,128)(2,1)} %param.17, bf16[474,512]{1,0:T(8,128)(2,1)S(1)} %copy-done, f32[512]{0:T(512)} %param.19), kind=kOutput, calls=%fused_computation.33 | convolution fusion | flops 14067302400 | bytes 57281024 | tf_op jit(solution)/shard_map/dot_general | solution.py:37
  32.8 13.5 %convolution_convert_fusion = bf16[28800,128]{1,0:T(8,128)(2,1)S(1)} fusion(bf16[28800,512]{1,0:T(8,128)(2,1)} %multiply_convert_fusion.1, bf16[512,128]{1,0:T(8,128)(2,1)S(1)} %copy-done.4), kind=kOutput, calls=%fused_computation.34 | convolution fusion | flops 3778560000 | bytes 36995072 | tf_op jit(solution)/shard_map/dot_general | solution.py:66
  52.5 5.8 %collective-permute-start.1 = (bf16[4,640,128]{2,1,0:T(8,128)(2,1)}, bf16[4,640,128]{2,1,0:T(8,128)(2,1)S(1)}, u32[]{:S(2)}, u32[]{:S(2)}) collective-permute-start(bf16[4,640,128]{2,1,0:T(8,128)(2,1)} %bitcast.2), channel_id=1, source_target_pairs={{4,0},{8,4},{12,8},{16,12},{20,16},{24,20},{28,24},{32,28},{36,32}... | collective-permute-start | bytes 1966088 | tf_op jit(solution)/shard_map/ppermute | solution.py:19
  64.8 15.0 %all-to-all-done = bf16[4,640,128]{1,2,0:T(8,128)(2,1)S(1)} async-done(((bf16[4,640,128]{1,2,0:T(8,128)(2,1)}), bf16[4,640,128]{1,2,0:T(8,128)(2,1)S(1)}, u32[]{:S(2)}, u32[]{:S(2)}) %all-to-all-start) | async-done | bytes 655392 | tf_op jit(solution)/shard_map/all_to_all | solution.py:76
  84.5 6.2 %bitcast_convert_fusion = f32[33920,128]{1,0:T(8,128)} fusion(bf16[53,640,128]{2,1,0:T(8,128)(2,1)S(1)} %pad_maximum_fusion), kind=kLoop, calls=%fused_computation.36 | loop fusion | flops 4341760 | bytes 26050560 | tf_op jit(solution)/shard_map/convert_element_type | solution.py:69
  90.7 231.8 %while.13 = (s32[]{:T(128)}, f32[640,128]{1,0:T(8,128)S(1)}, f32[640]{0:T(1024)S(1)}, s32[11,2048]{1,0:T(8,128)S(1)}, s32[11,2048]{1,0:T(8,128)S(1)}, /*index=5*...) while((s32[]{:T(128)}, f32[640,128]{1,0:T(8,128)S(1)}, ...), condition=%wide.region_2.3_spmd.clone, body=%wide.region_0.2_spmd.clone.sunk | while | flops 347021952 | bytes 7114884 | solution.py:117
  90.8 5.5 %gather_fusion = f32[2048,128]{1,0:T(8,128)S(1)} fusion(f32[640,128]{1,0:T(8,128)S(1)} %get-tuple-element.233, s32[2048]{0:T(1024)S(1)} %broadcast_clamp_fusion.4), kind=kCustom, calls=%fused_computation.1.clone.clone.1 | custom fusion | bytes 2105344 | tf_op jit(solution)/shard_map/while/body/eval_jaxpr/jit(_take)/gather | solution.py:89
  96.2 11.4 %gather_fusion.1 = f32[2048,128]{1,0:T(8,128)S(1)} fusion(f32[33920,128]{1,0:T(8,128)} %get-tuple-element.232, s32[2048]{0:T(1024)S(1)} %broadcast_clamp_fusion.5), kind=kCustom, calls=%fused_computation.clone.clone.1 | custom fusion | bytes 2105344 | tf_op jit(solution)/shard_map/while/body/eval_jaxpr/jit(_take)/gather | solution.py:89
  117.3 11.4 %gather_fusion.1 = f32[2048,128]{1,0:T(8,128)S(1)} fusion(f32[33920,128]{1,0:T(8,128)} %get-tuple-element.232, s32[2048]{0:T(1024)S(1)} %broadcast_clamp_fusion.5), kind=kCustom, calls=%fused_computation.clone.clone.1 | custom fusion | bytes 2105344 | tf_op jit(solution)/shard_map/while/body/eval_jaxpr/jit(_take)/gather | solution.py:89
  132.9 5.5 %gather_fusion = f32[2048,128]{1,0:T(8,128)S(1)} fusion(f32[640,128]{1,0:T(8,128)S(1)} %get-tuple-element.233, s32[2048]{0:T(1024)S(1)} %broadcast_clamp_fusion.4), kind=kCustom, calls=%fused_computation.1.clone.clone.1 | custom fusion | bytes 2105344 | tf_op jit(solution)/shard_map/while/body/eval_jaxpr/jit(_take)/gather | solution.py:89
  138.4 11.4 %gather_fusion.1 = f32[2048,128]{1,0:T(8,128)S(1)} fusion(f32[33920,128]{1,0:T(8,128)} %get-tuple-element.232, s32[2048]{0:T(1024)S(1)} %broadcast_clamp_fusion.5), kind=kCustom, calls=%fused_computation.clone.clone.1 | custom fusion | bytes 2105344 | tf_op jit(solution)/shard_map/while/body/eval_jaxpr/jit(_take)/gather | solution.py:89
  159.5 11.4 %gather_fusion.1 = f32[2048,128]{1,0:T(8,128)S(1)} fusion(f32[33920,128]{1,0:T(8,128)} %get-tuple-element.232, s32[2048]{0:T(1024)S(1)} %broadcast_clamp_fusion.5), kind=kCustom, calls=%fused_computation.clone.clone.1 | custom fusion | bytes 2105344 | tf_op jit(solution)/shard_map/while/body/eval_jaxpr/jit(_take)/gather | solution.py:89
  175.0 5.5 %gather_fusion = f32[2048,128]{1,0:T(8,128)S(1)} fusion(f32[640,128]{1,0:T(8,128)S(1)} %get-tuple-element.233, s32[2048]{0:T(1024)S(1)} %broadcast_clamp_fusion.4), kind=kCustom, calls=%fused_computation.1.clone.clone.1 | custom fusion | bytes 2105344 | tf_op jit(solution)/shard_map/while/body/eval_jaxpr/jit(_take)/gather | solution.py:89
  180.5 11.4 %gather_fusion.1 = f32[2048,128]{1,0:T(8,128)S(1)} fusion(f32[33920,128]{1,0:T(8,128)} %get-tuple-element.232, s32[2048]{0:T(1024)S(1)} %broadcast_clamp_fusion.5), kind=kCustom, calls=%fused_computation.clone.clone.1 | custom fusion | bytes 2105344 | tf_op jit(solution)/shard_map/while/body/eval_jaxpr/jit(_take)/gather | solution.py:89
  201.6 11.4 %gather_fusion.1 = f32[2048,128]{1,0:T(8,128)S(1)} fusion(f32[33920,128]{1,0:T(8,128)} %get-tuple-element.232, s32[2048]{0:T(1024)S(1)} %broadcast_clamp_fusion.5), kind=kCustom, calls=%fused_computation.clone.clone.1 | custom fusion | bytes 2105344 | tf_op jit(solution)/shard_map/while/body/eval_jaxpr/jit(_take)/gather | solution.py:89
  217.2 5.5 %gather_fusion = f32[2048,128]{1,0:T(8,128)S(1)} fusion(f32[640,128]{1,0:T(8,128)S(1)} %get-tuple-element.233, s32[2048]{0:T(1024)S(1)} %broadcast_clamp_fusion.4), kind=kCustom, calls=%fused_computation.1.clone.clone.1 | custom fusion | bytes 2105344 | tf_op jit(solution)/shard_map/while/body/eval_jaxpr/jit(_take)/gather | solution.py:89
  222.7 11.4 %gather_fusion.1 = f32[2048,128]{1,0:T(8,128)S(1)} fusion(f32[33920,128]{1,0:T(8,128)} %get-tuple-element.232, s32[2048]{0:T(1024)S(1)} %broadcast_clamp_fusion.5), kind=kCustom, calls=%fused_computation.clone.clone.1 | custom fusion | bytes 2105344 | tf_op jit(solution)/shard_map/while/body/eval_jaxpr/jit(_take)/gather | solution.py:89
  238.3 5.5 %gather_fusion = f32[2048,128]{1,0:T(8,128)S(1)} fusion(f32[640,128]{1,0:T(8,128)S(1)} %get-tuple-element.233, s32[2048]{0:T(1024)S(1)} %broadcast_clamp_fusion.4), kind=kCustom, calls=%fused_computation.1.clone.clone.1 | custom fusion | bytes 2105344 | tf_op jit(solution)/shard_map/while/body/eval_jaxpr/jit(_take)/gather | solution.py:89
  243.8 11.4 %gather_fusion.1 = f32[2048,128]{1,0:T(8,128)S(1)} fusion(f32[33920,128]{1,0:T(8,128)} %get-tuple-element.232, s32[2048]{0:T(1024)S(1)} %broadcast_clamp_fusion.5), kind=kCustom, calls=%fused_computation.clone.clone.1 | custom fusion | bytes 2105344 | tf_op jit(solution)/shard_map/while/body/eval_jaxpr/jit(_take)/gather | solution.py:89
  264.8 11.4 %gather_fusion.1 = f32[2048,128]{1,0:T(8,128)S(1)} fusion(f32[33920,128]{1,0:T(8,128)} %get-tuple-element.232, s32[2048]{0:T(1024)S(1)} %broadcast_clamp_fusion.5), kind=kCustom, calls=%fused_computation.clone.clone.1 | custom fusion | bytes 2105344 | tf_op jit(solution)/shard_map/while/body/eval_jaxpr/jit(_take)/gather | solution.py:89
  285.9 11.4 %gather_fusion.1 = f32[2048,128]{1,0:T(8,128)S(1)} fusion(f32[33920,128]{1,0:T(8,128)} %get-tuple-element.232, s32[2048]{0:T(1024)S(1)} %broadcast_clamp_fusion.5), kind=kCustom, calls=%fused_computation.clone.clone.1 | custom fusion | bytes 2105344 | tf_op jit(solution)/shard_map/while/body/eval_jaxpr/jit(_take)/gather | solution.py:89
  307.0 11.4 %gather_fusion.1 = f32[2048,128]{1,0:T(8,128)S(1)} fusion(f32[33920,128]{1,0:T(8,128)} %get-tuple-element.232, s32[2048]{0:T(1024)S(1)} %broadcast_clamp_fusion.5), kind=kCustom, calls=%fused_computation.clone.clone.1 | custom fusion | bytes 2105344 | tf_op jit(solution)/shard_map/while/body/eval_jaxpr/jit(_take)/gather | solution.py:89
  329.0 17.0 %all-to-all-done.1 = f32[4,640,128]{1,2,0:T(8,128)S(1)} async-done(((f32[4,640,128]{1,2,0:T(8,128)}), f32[4,640,128]{1,2,0:T(8,128)S(1)}, u32[]{:S(2)}, u32[]{:S(2)}) %all-to-all-start.1) | async-done | bytes 1310752 | tf_op jit(solution)/shard_map/all_to_all | solution.py:31
  346.3 7.5 %all-reduce = (f32[640,1]{0,1:T(1,128)S(1)}, f32[640,1]{0,1:T(1,128)S(1)}) all-reduce(f32[640,1]{0,1:T(1,128)S(1)} %broadcast_in_dim.39, f32[640,1]{0,1:T(1,128)S(1)} %broadcast_in_dim.40), channel_id=1, replica_groups=mesh['lon'=32,'ch'=4] {'ch'}, use_global_device_ids=true, to_apply=%region_5.6 | all-reduce | flops 1280 | bytes 10240 | tf_op jit(solution)/shard_map/psum | solution.py:123
  (145 shorter events, 104.2 us)
Async XLA Ops:
  0.0 1.0 copy-start
  0.0 32.8 %copy-start.4 = (bf16[512,128]{1,0:T(8,128)(2,1)S(1)}, bf16[512,128]{1,0:T(8,128)(2,1)}, u32[]{:S(2)}) copy-start(bf16[512,128]{1,0:T(8,128)(2,1)} %param.24) | copy-start | bytes 393220
  32.8 25.5 %copy-start.3 = (bf16[640,128]{1,0:T(8,128)(2,1)S(1)}, bf16[640,128]{1,0:T(8,128)(2,1)}, u32[]{:S(2)}) copy-start(bf16[640,128]{1,0:T(8,128)(2,1)} %param.20) | copy-start | bytes 491524
  32.8 31.7 %copy-start.7 = (s32[22528]{0:T(1024)S(1)}, s32[22528]{0:T(1024)}, u32[]{:S(2)}) copy-start(s32[22528]{0:T(1024)} %param.23) | copy-start | bytes 270340
  32.8 31.8 %copy-start.8 = (s32[22528]{0:T(1024)S(1)}, s32[22528]{0:T(1024)}, u32[]{:S(2)}) copy-start(s32[22528]{0:T(1024)} %param.22) | copy-start | bytes 270340
  32.8 47.0 %copy-start.5 = (bf16[512,128]{1,0:T(8,128)(2,1)S(1)}, bf16[512,128]{1,0:T(8,128)(2,1)}, u32[]{:S(2)}) copy-start(bf16[512,128]{1,0:T(8,128)(2,1)} %param.25) | copy-start | bytes 393220
  46.3 3.0 copy-start.2
  50.5 29.7 %collective-permute-start = (bf16[4,640,128]{2,1,0:T(8,128)(2,1)}, bf16[4,640,128]{2,1,0:T(8,128)(2,1)S(1)}, u32[]{:S(2)}, u32[]{:S(2)}) collective-permute-start(bf16[4,640,128]{2,1,0:T(8,128)(2,1)} %bitcast), channel_id=1, source_target_pairs={{0,4},{4,8},{8,12},{12,16},{16,20},{20,24},{24,28},{28,32},{32,36}... | collective-permute-start | bytes 1966088 | tf_op jit(solution)/shard_map/ppermute | solution.py:16
  52.5 27.7 %collective-permute-start.1 = (bf16[4,640,128]{2,1,0:T(8,128)(2,1)}, bf16[4,640,128]{2,1,0:T(8,128)(2,1)S(1)}, u32[]{:S(2)}, u32[]{:S(2)}) collective-permute-start(bf16[4,640,128]{2,1,0:T(8,128)(2,1)} %bitcast.2), channel_id=1, source_target_pairs={{4,0},{8,4},{12,8},{16,12},{20,16},{24,20},{28,24},{32,28},{36,32}... | collective-permute-start | bytes 1966088 | tf_op jit(solution)/shard_map/ppermute | solution.py:19
  59.4 20.4 %all-to-all-start = ((bf16[4,640,128]{1,2,0:T(8,128)(2,1)}), bf16[4,640,128]{1,2,0:T(8,128)(2,1)S(1)}, u32[]{:S(2)}, u32[]{:S(2)}) async-start(bf16[4,640,128]{1,2,0:T(8,128)(2,1)} %stack.2), calls=%async_computation | async-start | bytes 1310720 | tf_op jit(solution)/shard_map/all_to_all | solution.py:76
  84.5 6.2 %copy-start.11 = (bf16[4,128]{1,0:T(4,128)(2,1)S(1)}, bf16[4,128]{1,0:T(4,128)(2,1)}, u32[]{:S(2)}) copy-start(bf16[4,128]{1,0:T(4,128)(2,1)} %param.26) | copy-start | bytes 3076
  84.5 6.2 %copy-start.12 = (f32[128]{0:T(128)S(1)}, f32[128]{0:T(128)}, u32[]{:S(2)}) copy-start(f32[128]{0:T(128)} %param.27) | copy-start | bytes 1540
  90.7 231.8 %copy-start.6 = (bf16[128,512]{1,0:T(8,128)(2,1)S(1)}, bf16[128,512]{1,0:T(8,128)(2,1)}, u32[]{:S(2)}) copy-start(bf16[128,512]{1,0:T(8,128)(2,1)} %param.28) | copy-start | bytes 393220
  90.7 263.2 %copy-start.9 = (f32[128]{0:T(128)S(1)}, f32[128]{0:T(128)}, u32[]{:S(2)}) copy-start(f32[128]{0:T(128)} %param.31) | copy-start | bytes 1540
  90.7 263.2 %copy-start.10 = (f32[128]{0:T(128)S(1)}, f32[128]{0:T(128)}, u32[]{:S(2)}) copy-start(f32[128]{0:T(128)} %param.30) | copy-start | bytes 1540
  322.5 32.4 %copy-start.1 = (bf16[474,512]{1,0:T(8,128)(2,1)S(1)}, bf16[474,512]{1,0:T(8,128)(2,1)}, u32[]{:S(2)}) copy-start(bf16[474,512]{1,0:T(8,128)(2,1)} %param.18) | copy-start | bytes 1456132
  324.3 21.7 %all-to-all-start.1 = ((f32[4,640,128]{1,2,0:T(8,128)}), f32[4,640,128]{1,2,0:T(8,128)S(1)}, u32[]{:S(2)}, u32[]{:S(2)}) async-start(f32[4,640,128]{1,2,0:T(8,128)} %bitcast.9), calls=%async_computation.1 | async-start | bytes 2621440 | tf_op jit(solution)/shard_map/all_to_all | solution.py:31
